TPU v7x, 128 devices: a whole 4x4x4 slice. The times are simulated.
128 devices in a mesh: gz: 64 (over y, x, z_hi, core), gy: 2 (over z_lo).
Axes of the slice: x: 4, y: 4, z: 4 (z_hi: 2, z_lo: 2; z = z_hi * 2 + z_lo), core: 2. Of those that a mesh axis runs over, the one named last changes fastest.
Arguments:
- snapshots: float32 [48, 256, 128, 256], P(None, 'gz', 'gy'), may hold values from -6 to 6
- energies: float32 [48], replicated, may hold values from 0.3 to 3
- plane_weight: float32 [256], P('gz'), may hold values from 1 to 10
Outputs:
- modes: float32 [16, 256, 128, 256], P(None, 'gz', 'gy')
- basis: float32 [48, 16], replicated
All inputs are finite; a program needn't handle non-finite values.
Results may differ from a plain program's by a relative error of at most 0.0003.
Values sent between devices are 32-bit elements; how exact they have to be, the bound alone decides.
A program may use at most 128 MiB of HBM per device.

v0:
```python
import functools

import jax
import jax.numpy as jnp
from jax import lax
from jax.sharding import Mesh
from jax.sharding import PartitionSpec as P

MODES = 16
ITERS = 6
GZ = ("gz_0", "gz_1", "gz_2", "gz_3")
GZ_GY = ("gz_0", "gz_1", "gz_2", "gz_3", "gy")


def padded_2(block, sides, width):
    for axis, dim in sides:
        count = lax.axis_size(axis)
        forward = [(i, i + 1) for i in range(count - 1)]
        forward.append((count - 1, 0))
        backward = [(target, source) for source, target in forward]
        low = lax.ppermute(
            lax.slice_in_dim(block, block.shape[dim] - width, None, axis=dim), axis, forward
        )
        high = lax.ppermute(lax.slice_in_dim(block, 0, width, axis=dim), axis, backward)
        block = jnp.concatenate([low, block, high], axis=dim)
    return block


def one_axis_at_a_time(x, axes):
    return functools.reduce(lax.psum, axes, x)


def local(snapshots, energies, plane_weight):
    count, planes, rows, width = snapshots.shape
    total = planes * lax.axis_size(GZ) * rows * lax.axis_size("gy") * width
    scaled = snapshots * energies[:, None, None, None]
    padded = padded_2(scaled, ((GZ, 1),), 1)
    filtered = 0.25 * padded[:, :-2] + 0.5 * scaled + 0.25 * padded[:, 2:]
    flat = filtered.reshape(count, -1)
    weighted = (filtered * plane_weight[None, :, None, None]).reshape(count, -1)
    partial_value = jnp.dot(weighted, flat.T, precision=lax.Precision.HIGHEST) / total
    gram = one_axis_at_a_time(partial_value, GZ_GY)
    basis = jnp.eye(count, dtype=jnp.float32)[:, :MODES]
    for step in range(ITERS):
        image = jnp.dot(gram, basis, precision=lax.Precision.HIGHEST)
        factor = jnp.linalg.cholesky(jnp.dot(image.T, image, precision=lax.Precision.HIGHEST))
        basis = jax.scipy.linalg.solve_triangular(factor, image.T, lower=True).T
    raw = jnp.dot(basis.T, flat, precision=lax.Precision.HIGHEST).reshape(
        MODES, planes, rows, width
    )
    projected = jnp.dot(gram, basis, precision=lax.Precision.HIGHEST)
    norms = jnp.sum(basis * projected, axis=0)
    modes = raw / jnp.sqrt(norms)[:, None, None, None]
    return (modes, basis)


def solution(mesh):
    torus = Mesh(
        mesh.devices.reshape(4, 4, 2, 2, mesh.shape["gy"]), ("gz_0", "gz_1", "gz_2", "gz_3", "gy")
    )
    in_specs = (P(None, GZ, "gy", None), P(), P(GZ))
    out_specs = (P(None, GZ, "gy", None), P())
    return jax.shard_map(local, mesh=torus, in_specs=in_specs, out_specs=out_specs, check_vma=False)
```

profile of v0, /device:TPU:0, one launch (start us, length us, event | category | flops | bytes accessed | tf_op | source)
XLA Modules:
  0.0 242.3 jit_solution(10219474833716640142)
XLA Ops:
  0.6 12.0 %broadcast_multiply_fusion.1 = f32[48,4,64,256]{3,2,1,0:T(8,128)} fusion(f32[48,4,64,256]{3,2,1,0:T(8,128)} %param.6, f32[48]{0:T(128)} %param.7), kind=kLoop, calls=%fused_computation.12 | loop fusion | flops 3145728 | bytes 25166016 | tf_op jit(solution)/shard_map/mul | solution.py:36
  12.7 3.7 %fusion.67 = (f32[48,1,64,256]{3,2,1,0:T(8,128)S(1)}, f32[48,1,64,256]{3,2,1,0:T(8,128)S(1)}) fusion(f32[48,4,64,256]{3,2,1,0:T(8,128)} %broadcast_multiply_fusion.1), kind=kLoop, calls=%fused_computation.84 | loop fusion | bytes 12582912 | tf_op jit(solution)/shard_map/slice | solution.py:22
  16.5 8.1 %collective-permute-start.1 = (f32[48,1,64,256]{3,2,1,0:T(8,128)S(1)}, f32[48,1,64,256]{3,2,1,0:T(8,128)}, u32[]{:S(2)}, u32[]{:S(2)}) collective-permute-start(f32[48,1,64,256]{3,2,1,0:T(8,128)S(1)} %get-tuple-element.11), channel_id=1, source_target_pairs={{2,0},{4,2},{6,4},{8,6},{10,8},{12,10},{14,12},{16,14},{18,16},{20... | collective-permute-start | bytes 9437192 | tf_op jit(solution)/shard_map/ppermute | solution.py:24
  24.6 35.1 %collective-permute-done = f32[48,1,64,256]{3,2,1,0:T(8,128)} collective-permute-done((f32[48,1,64,256]{3,2,1,0:T(8,128)S(1)}, f32[48,1,64,256]{3,2,1,0:T(8,128)}, u32[]{:S(2)}, u32[]{:S(2)}) %collective-permute-start) | collective-permute-done | bytes 3145760 | tf_op jit(solution)/shard_map/ppermute | solution.py:21
  59.7 13.5 %broadcast_multiply_fusion = (f32[48,4,64,256]{3,2,1,0:T(8,128)}, f32[48,4,64,256]{3,2,1,0:T(8,128)}) fusion(f32[4]{0:T(128)S(1)} %copy-done.2, f32[48,1,64,256]{3,2,1,0:T(8,128)} %collective-permute-done.1, f32[48,4,64,256]{3,2,1,0:T(8,128)S(1)} %copy-done, f32[48,1,64,256]{3,2,1,0:T(8,128)} %collective-permute-done), kind=kLoop, calls=%fused_computation.11 | loop fusion | flops 25165824 | bytes 44040208 | tf_op jit(solution)/shard_map/mul | solution.py:40
  73.2 32.1 %fusion.16 = f32[48,48]{1,0:T(8,128)S(1)} fusion(f32[48,4,64,256]{3,2,1,0:T(8,128)} %get-tuple-element.9, f32[48,4,64,256]{3,2,1,0:T(8,128)} %get-tuple-element.8), kind=kOutput, calls=%fused_computation.15 | convolution fusion | flops 1811941632 | bytes 25175040 | tf_op jit(solution)/shard_map/dot_general | solution.py:41
  105.3 15.6 %psum.35 = f32[48,48]{1,0:T(8,128)S(1)} all-reduce(f32[48,48]{1,0:T(8,128)S(1)} %fusion.16), channel_id=1, replica_groups=mesh['gz_0'=4,'gz_1'=4,'gz_2'=2,'gz_3'=2,'gy'=2] {'gz_0'}, use_global_device_ids=true, to_apply=%region_0.0 | all-reduce | flops 2304 | bytes 18432 | tf_op jit(solution)/shard_map/psum | solution.py:30
  120.9 14.9 %psum.36 = f32[48,48]{1,0:T(8,128)S(1)} all-reduce(f32[48,48]{1,0:T(8,128)S(1)} %psum.35), channel_id=1, replica_groups=mesh['gz_0'=4,'gz_1'=4,'gz_2'=2,'gz_3'=2,'gy'=2] {'gz_1'}, use_global_device_ids=true, to_apply=%region_1.0 | all-reduce | flops 2304 | bytes 18432 | tf_op jit(solution)/shard_map/psum | solution.py:30
  135.8 44.9 %psum.37 = f32[48,48]{1,0:T(8,128)S(1)} all-reduce(f32[48,48]{1,0:T(8,128)S(1)} %psum.36), channel_id=1, replica_groups=mesh['gz_0'=4,'gz_1'=4,'gz_2'=2,'gz_3'=2,'gy'=2] {'gz_2'}, use_global_device_ids=true, to_apply=%region_2.0 | all-reduce | flops 2304 | bytes 18432 | tf_op jit(solution)/shard_map/psum | solution.py:30
  180.7 3.4 %psum.38 = f32[48,48]{1,0:T(8,128)S(1)} all-reduce(f32[48,48]{1,0:T(8,128)S(1)} %psum.37), channel_id=1, replica_groups=mesh['gz_0'=4,'gz_1'=4,'gz_2'=2,'gz_3'=2,'gy'=2] {'gz_3'}, use_global_device_ids=true, to_apply=%region_3.0 | all-reduce | flops 2304 | bytes 18432 | tf_op jit(solution)/shard_map/psum | solution.py:30
  184.1 7.8 %psum.39 = f32[48,48]{1,0:T(8,128)S(1)} all-reduce(f32[48,48]{1,0:T(8,128)S(1)} %psum.38), channel_id=1, replica_groups=mesh['gz_0'=4,'gz_1'=4,'gz_2'=2,'gz_3'=2,'gy'=2] {'gy'}, use_global_device_ids=true, to_apply=%region_4.0 | all-reduce | flops 2304 | bytes 18432 | tf_op jit(solution)/shard_map/psum | solution.py:30
  191.9 0.2 fusion.22
  192.3 1.5 cholesky.104
  193.8 0.6 compare_reduce_fusion.5
  194.5 0.6 fusion.24
  195.1 1.2 custom-call.10
  196.3 0.2 fusion.51
  196.5 0.2 fusion.69
  196.9 1.5 cholesky.115
  198.4 0.6 compare_reduce_fusion.4
  199.1 0.6 fusion.25
  199.7 1.2 custom-call.11
  201.0 0.2 fusion.47
  201.2 0.2 fusion.71
  201.5 1.5 cholesky.126
  203.0 0.6 compare_reduce_fusion.3
  203.7 0.6 fusion.26
  204.4 1.2 custom-call.12
  205.6 0.2 fusion.43
  205.8 0.2 fusion.73
  206.2 1.5 cholesky.137
  207.7 0.6 compare_reduce_fusion.2
  208.3 0.6 fusion.27
  209.0 1.2 custom-call.13
  210.2 0.2 fusion.39
  210.8 1.5 cholesky.148
  212.3 0.6 compare_reduce_fusion.1
  212.9 0.6 fusion.28
  213.6 1.2 custom-call.14
  214.8 0.2 fusion.35
  215.4 1.5 cholesky.159
  216.9 0.6 compare_reduce_fusion
  217.6 0.6 fusion.29
  218.2 1.2 custom-call.15
  219.4 0.2 fusion.31
  219.7 0.3 fusion.21
  220.0 17.9 %broadcast_divide_fusion = f32[16,4,64,256]{3,0,2,1:T(8,128)S(1)} fusion(f32[16]{0:T(128)S(1)} %sqrt.7, f32[4,64,256,48]{2,1,0,3:T(8,128)} %bitcast.120, f32[16,48]{1,0:T(8,128)S(1)} %fusion.31), kind=kOutput, calls=%fused_computation.13 | convolution fusion | flops 605028352 | bytes 16780352 | tf_op jit(solution)/shard_map/dot_general | solution.py:48
  237.9 4.4 %copy.23 = f32[16,4,64,256]{3,2,1,0:T(8,128)} copy(f32[16,4,64,256]{3,0,2,1:T(8,128)S(1)} %broadcast_divide_fusion) | data formatting | bytes 8388608
  (35 shorter events, 1.9 us)
Async XLA Ops:
  12.7 47.1 %copy-start = (f32[48,4,64,256]{3,2,1,0:T(8,128)S(1)}, f32[48,4,64,256]{3,2,1,0:T(8,128)}, u32[]{:S(2)}) copy-start(f32[48,4,64,256]{3,2,1,0:T(8,128)} %broadcast_multiply_fusion.1) | copy-start | bytes 37748740
  12.7 47.1 %copy-start.2 = (f32[4]{0:T(128)S(1)}, f32[4]{0:T(128)}, u32[]{:S(2)}) copy-start(f32[4]{0:T(128)} %param.8) | copy-start | bytes 52
  16.4 43.3 %collective-permute-start = (f32[48,1,64,256]{3,2,1,0:T(8,128)S(1)}, f32[48,1,64,256]{3,2,1,0:T(8,128)}, u32[]{:S(2)}, u32[]{:S(2)}) collective-permute-start(f32[48,1,64,256]{3,2,1,0:T(8,128)S(1)} %get-tuple-element.10), channel_id=1, source_target_pairs={{0,2},{2,4},{4,6},{6,8},{8,10},{10,12},{12,14},{14,16},{16,18},{18... | collective-permute-start | bytes 9437192 | tf_op jit(solution)/shard_map/ppermute | solution.py:21
  16.5 43.2 %collective-permute-start.1 = (f32[48,1,64,256]{3,2,1,0:T(8,128)S(1)}, f32[48,1,64,256]{3,2,1,0:T(8,128)}, u32[]{:S(2)}, u32[]{:S(2)}) collective-permute-start(f32[48,1,64,256]{3,2,1,0:T(8,128)S(1)} %get-tuple-element.11), channel_id=1, source_target_pairs={{2,0},{4,2},{6,4},{8,6},{10,8},{12,10},{14,12},{16,14},{18,16},{20... | collective-permute-start | bytes 9437192 | tf_op jit(solution)/shard_map/ppermute | solution.py:24
  219.7 22.7 %copy-start.1 = (f32[16,48]{1,0:T(8,128)}, f32[16,48]{1,0:T(8,128)S(1)}, u32[]{:S(2)}) copy-start(f32[16,48]{1,0:T(8,128)S(1)} %fusion.31) | copy-start | bytes 9220
where the time goes:
time: 243 us; the launch traced here: 242 us
  blocking collectives  86.6 us (36%)
  matrix products  53.4 us (22%)
  other arithmetic  49.7 us (20%)
  waiting for transfers between devices  35.1 us (14%)
  local copies, waits for them, and re-layouts  8.63 us (4%)
  starting transfers between devices  8.22 us (3%)
    psum x5, blocking collectives, one_axis_at_a_time(): return functools.reduce(lax.psum, axes, x)  86.6 us
    ppermute x1, waiting for transfers between devices, padded_2(): lax.ppermute(lax.slice_in_dim(block, block.shape[dim] - width, None, axis...  35.1 us
    dot_general x1, matrix products, local(): jnp.dot(weighted, flat.T, precision=lax.Precision.HIGHEST) / total  32.1 us
    dot_general x1, matrix products, local(): jnp.dot(basis.T, flat, precision=lax.Precision.HIGHEST)  17.9 us
    mul x1, other arithmetic, local(): weighted = (filtered * plane_weight[None, :, None, None]).reshape(count, -1)  13.5 us
    another operation x18, other arithmetic, local(): jnp.linalg.cholesky(jnp.dot(image.T, image, precision=lax.Precision.HIGHE...  12.9 us
    mul x1, other arithmetic, local(): scaled = snapshots * energies[:, None, None, None]  12 us
    another operation x12, other arithmetic, local(): basis = jax.scipy.linalg.solve_triangular(factor, image.T, lower=True).T  11.3 us
  transfers between devices with their start and end apart: 2, of which 1 were waited for; matrix products, arithmetic and copies ran while one was open for 0% of the time, Pallas kernels for 0%

commit v1 on v0

v1 whole, which is shorter than its diff:
```python
import functools

import jax
import jax.numpy as jnp
from jax import lax
from jax.experimental import pallas as pl
from jax.experimental.pallas import tpu as pltpu
from jax.sharding import Mesh
from jax.sharding import PartitionSpec as P

MODES = 16
ITERS = 6
NAMES = ("gz_y", "gz_x", "gz_h", "gz_c", "gy")
GZ = NAMES[:4]
MESH = pl.DeviceIdType.MESH
HIGH = lax.Precision.HIGHEST
F32 = jnp.float32
BF16 = jnp.bfloat16
ROWS = 8


def nt(a, b, precision=None):
    return lax.dot_general(
        a, b, (((1,), (1,)), ((), ())), precision=precision, preferred_element_type=F32
    )


def line_device(index):
    return {"gz_h": index // 4, "gz_c": (index // 2) % 2, "gy": index % 2}


def plane_device(index):
    return {"gz_y": index // 4, "gz_x": index % 4}


def slab_device(index):
    return {
        "gz_y": index // 16,
        "gz_x": (index // 4) % 4,
        "gz_h": (index // 2) % 2,
        "gz_c": index % 2,
    }


def split(x):
    high = x.astype(BF16)
    return high, (x - high.astype(F32)).astype(BF16)


def gram_kernel(
    chunks,
    snap,
    weight,
    filt_out,
    gram_out,
    field,
    below,
    above,
    filt,
    total,
    weights,
    line_buf,
    plane_buf,
    load_sem,
    small_sem,
    store_sem,
    halo_send,
    halo_recv,
    line_send,
    line_recv,
    plane_send,
    plane_recv,
):
    count = field.shape[2]
    tall = count * ROWS
    y, x, h, c, g = (lax.axis_index(name) for name in NAMES)
    slab = ((y * 4 + x) * 2 + h) * 2 + c
    slabs = 64
    upper = slab_device(lax.rem(slab + 1, slabs))
    lower = slab_device(lax.rem(slab + slabs - 1, slabs))
    line = (h * 2 + c) * 2 + g
    plane = y * 4 + x

    barrier = pltpu.get_barrier_semaphore()
    for device in (upper, lower):
        pl.semaphore_signal(barrier, inc=1, device_id=device, device_id_type=MESH)
    for step in range(1, 8):
        device = line_device(lax.rem(line + step, 8))
        pl.semaphore_signal(barrier, inc=1, device_id=device, device_id_type=MESH)
    for step in range(1, 16):
        device = plane_device(lax.rem(plane + step, 16))
        pl.semaphore_signal(barrier, inc=1, device_id=device, device_id_type=MESH)

    def load(chunk, z):
        rows = pl.ds(pl.multiple_of(chunk * ROWS, ROWS), ROWS)
        return pltpu.make_async_copy(
            snap.at[:, z, rows, :], field.at[chunk, z], load_sem.at[chunk, z]
        )

    def halo(chunk, side):
        rows = pl.ds(pl.multiple_of(chunk * ROWS, ROWS), ROWS)
        return pltpu.make_async_remote_copy(
            src_ref=snap.at[:, 3 if side == 0 else 0, rows, :],
            dst_ref=(below if side == 0 else above).at[chunk],
            send_sem=halo_send.at[side, chunk],
            recv_sem=halo_recv.at[side, chunk],
            device_id=upper if side == 0 else lower,
            device_id_type=MESH,
        )

    def store(chunk, z):
        return pltpu.make_async_copy(
            filt.at[z, chunk], filt_out.at[z, chunk], store_sem.at[chunk, z]
        )

    pl.semaphore_wait(barrier, 24)
    for chunk in range(chunks):
        for side in range(2):
            halo(chunk, side).start()
    read = pltpu.make_async_copy(weight, weights, small_sem)
    read.start()
    for chunk in range(chunks):
        for z in range(4):
            load(chunk, z).start()
    read.wait()
    root = [jnp.sqrt(jnp.full((1, 256), weights[z], F32)) for z in range(4)]
    total[...] = jnp.zeros_like(total)

    def smooth(a, b, c, z):
        value = (0.25 * root[z]) * (a + c) + (0.5 * root[z]) * b
        return value

    def accumulate(chunk, planes, values):
        highs, lows = [], []
        for z, value in zip(planes, values):
            high, low = split(value)
            filt[z, chunk, :tall, :] = high
            filt[z, chunk, tall:, :] = low
            highs.append(high)
            lows.append(low)
        high = jnp.concatenate(highs, axis=1)
        low = jnp.concatenate(lows, axis=1)
        total[:, :tall] += nt(high, high)
        total[:, tall:] += nt(high, low)
        for z in planes:
            store(chunk, z).start()

    def flat(ref):
        return ref[...].reshape(tall, ref.shape[-1])

    def inner(chunk, carry):
        for z in range(4):
            load(chunk, z).wait()
        s = [flat(field.at[chunk, z]) for z in range(4)]
        accumulate(
            chunk, (1, 2), [smooth(s[0], s[1], s[2], 1), smooth(s[1], s[2], s[3], 2)]
        )
        return carry

    lax.fori_loop(0, chunks, inner, 0)

    def outer(chunk, carry):
        for side in range(2):
            halo(chunk, side).wait_recv()
        first = smooth(
            flat(below.at[chunk]), flat(field.at[chunk, 0]), flat(field.at[chunk, 1]), 0
        )
        last = smooth(
            flat(field.at[chunk, 2]), flat(field.at[chunk, 3]), flat(above.at[chunk]), 3
        )
        accumulate(chunk, (0, 3), [first, last])
        return carry

    lax.fori_loop(0, chunks, outer, 0)

    whole = total[:, :tall] + 2.0 * total[:, tall:]
    keep = lax.broadcasted_iota(jnp.int32, (tall, tall), 0) % ROWS == (
        lax.broadcasted_iota(jnp.int32, (tall, tall), 1) % ROWS
    )
    picked = jnp.sum(jnp.where(keep, whole, 0.0).reshape(count, ROWS, tall), axis=1)
    half = count // 2
    wide = jnp.concatenate([picked[:half], picked[half:]], axis=1)
    place = lax.broadcasted_iota(jnp.int32, (128, 2 * tall), 1) // ROWS
    place = jnp.where(place < count, place, place - count + 64)
    choose = (place == lax.broadcasted_iota(jnp.int32, (128, 2 * tall), 0)).astype(F32)
    packed = nt(wide, choose, HIGH)

    def reduce(value, buf, me, size, device_of, send, recv):
        buf[me] = value
        copies = []
        for step in range(1, size):
            other = lax.rem(me + step, size)
            copies.append(
                pltpu.make_async_remote_copy(
                    src_ref=buf.at[me],
                    dst_ref=buf.at[me],
                    send_sem=send.at[other],
                    recv_sem=recv.at[me],
                    device_id=device_of(other),
                    device_id_type=MESH,
                )
            )
        for copy in copies:
            copy.start()
        for step in range(1, size):
            other = lax.rem(me + step, size)
            pltpu.make_async_remote_copy(
                src_ref=buf.at[other],
                dst_ref=buf.at[other],
                send_sem=send.at[other],
                recv_sem=recv.at[other],
                device_id=device_of(other),
                device_id_type=MESH,
            ).wait_recv()
        parts = [buf[i] for i in range(size)]
        while len(parts) > 1:
            parts = [parts[i] + parts[i + 1] for i in range(0, len(parts), 2)]
        return parts[0], copies

    packed, line_copies = reduce(
        packed, line_buf, line, 8, line_device, line_send, line_recv
    )
    packed, plane_copies = reduce(
        packed, plane_buf, plane, 16, plane_device, plane_send, plane_recv
    )
    gram_out[...] = packed
    for copy in line_copies + plane_copies:
        copy.wait_send()
    for chunk in range(chunks):
        for side in range(2):
            halo(chunk, side).wait_send()
        for z in range(4):
            store(chunk, z).wait()


def mode_kernel(
    chunks,
    cells,
    packed,
    energy_row,
    energy_col,
    weight,
    filt_in,
    modes_out,
    basis_out,
    filt,
    modes,
    columns,
    lines,
    load_sem,
    store_sem,
):
    count = energy_row.shape[1]
    tall = count * ROWS

    def load(chunk, z):
        return pltpu.make_async_copy(
            filt_in.at[z, chunk], filt.at[z, chunk], load_sem.at[z, chunk]
        )

    def store(chunk, z):
        rows = pl.ds(pl.multiple_of(chunk * ROWS, ROWS), ROWS)
        return pltpu.make_async_copy(
            modes.at[z, chunk], modes_out.at[:, z, rows, :], store_sem.at[z, chunk]
        )

    for z in range(4):
        for chunk in range(chunks):
            load(chunk, z).start()

    half = count // 2
    value = packed[...]
    gram = jnp.concatenate([value[:, :count], value[:, 64 : 64 + count]], axis=0)
    gram = 0.5 * (gram + gram.T)
    gram = gram * (energy_col[...] * energy_row[...]) / cells

    eye = (
        lax.broadcasted_iota(jnp.int32, (MODES, count), 0)
        == lax.broadcasted_iota(jnp.int32, (MODES, count), 1)
    ).astype(F32)

    def iterate(step, basis):
        image = jnp.dot(basis, gram, precision=HIGH, preferred_element_type=F32)
        square = nt(image, image, HIGH)
        for j in range(MODES):
            columns[j] = jnp.broadcast_to(square[:, j : j + 1], (MODES, 128))
        lines[:, :count] = image
        entry = {
            (i, j): columns[j, i : i + 1, :] for j in range(MODES) for i in range(j, MODES)
        }
        row = [lines[i : i + 1, :] for i in range(MODES)]
        for k in range(MODES):
            scale = lax.rsqrt(entry[k, k])
            inverse = scale * scale
            row[k] = row[k]
            factors = {i: entry[i, k] * inverse for i in range(k + 1, MODES)}
            for i in range(k + 1, MODES):
                row[i] = row[i] - factors[i] * row[k]
                for j in range(k + 1, i + 1):
                    entry[i, j] = entry[i, j] - factors[i] * entry[j, k]
            row[k] = row[k] * scale
        for i in range(MODES):
            lines[i : i + 1, :] = row[i]
        return lines[:, :count]

    lines[...] = jnp.zeros_like(lines)
    basis = lax.fori_loop(0, ITERS, iterate, eye)
    basis_out[...] = basis.T
    projected = jnp.dot(basis, gram, precision=HIGH, preferred_element_type=F32)
    norms = jnp.sum(basis * projected, axis=1, keepdims=True)
    scaled = basis * energy_row[...] * lax.rsqrt(norms)
    high, low = split(scaled)
    both = jnp.concatenate([high.astype(F32), low.astype(F32)], axis=0).astype(BF16)
    spread = (
        lax.broadcasted_iota(jnp.int32, (count, tall), 0)
        == lax.broadcasted_iota(jnp.int32, (count, tall), 1) // ROWS
    ).astype(BF16)
    both = jnp.dot(both, spread, preferred_element_type=F32).astype(BF16)
    tallest = 2 * MODES * ROWS
    repeat = (
        lax.broadcasted_iota(jnp.int32, (tallest, 2 * MODES), 0) // ROWS
        == lax.broadcasted_iota(jnp.int32, (tallest, 2 * MODES), 1)
    ).astype(BF16)
    both = jnp.dot(repeat, both, preferred_element_type=F32)
    keep = lax.broadcasted_iota(jnp.int32, (tallest, tall), 0) % ROWS == (
        lax.broadcasted_iota(jnp.int32, (tallest, tall), 1) % ROWS
    )
    both = jnp.where(keep, both, 0.0).astype(BF16)
    top, bottom = both[: MODES * ROWS], both[MODES * ROWS :]

    for z in range(4):
        back = lax.rsqrt(jnp.full((1, 256), weight[z], F32))

        def project(chunk, carry, z=z, back=back):
            load(chunk, z).wait()
            high = filt[z, chunk, :tall, :]
            low = filt[z, chunk, tall:, :]
            raw = jnp.dot(top, high, preferred_element_type=F32)
            raw += jnp.dot(top, low, preferred_element_type=F32)
            raw += jnp.dot(bottom, high, preferred_element_type=F32)
            modes[z, chunk] = (raw * back).reshape(MODES, ROWS, raw.shape[-1])
            store(chunk, z).start()
            return carry

        lax.fori_loop(0, chunks, project, 0)
    for z in range(4):
        for chunk in range(chunks):
            store(chunk, z).wait()


def local(snapshots, energies, plane_weight):
    count, planes, rows, width = snapshots.shape
    chunks = rows // ROWS
    tall = count * ROWS
    any_space = pl.BlockSpec(memory_space=pl.ANY)
    vmem = pl.BlockSpec(memory_space=pltpu.VMEM)
    smem = pl.BlockSpec(memory_space=pltpu.SMEM)
    dma = pltpu.SemaphoreType.DMA
    filt_shape = (planes, chunks, 2 * tall, width)
    filt, packed = pl.pallas_call(
        functools.partial(gram_kernel, chunks),
        name="gram",
        out_shape=(
            jax.ShapeDtypeStruct(filt_shape, BF16),
            jax.ShapeDtypeStruct((count // 2, 128), F32),
        ),
        in_specs=[any_space, any_space],
        out_specs=(any_space, vmem),
        scratch_shapes=[
            pltpu.VMEM((chunks, planes, count, ROWS, width), F32),
            pltpu.VMEM((chunks, count, ROWS, width), F32),
            pltpu.VMEM((chunks, count, ROWS, width), F32),
            pltpu.VMEM(filt_shape, BF16),
            pltpu.VMEM((tall, 2 * tall), F32),
            pltpu.SMEM((planes,), F32),
            pltpu.VMEM((8, count // 2, 128), F32),
            pltpu.VMEM((16, count // 2, 128), F32),
            dma((chunks, planes)),
            dma,
            dma((chunks, planes)),
            dma((2, chunks)),
            dma((2, chunks)),
            dma((8,)),
            dma((8,)),
            dma((16,)),
            dma((16,)),
        ],
        compiler_params=pltpu.CompilerParams(
            collective_id=0, has_side_effects=True, vmem_limit_bytes=60 * 2**20
        ),
    )(snapshots, plane_weight)
    cells = planes * 64 * rows * 2 * width
    modes, basis = pl.pallas_call(
        functools.partial(mode_kernel, chunks, cells),
        name="modes",
        out_shape=(
            jax.ShapeDtypeStruct((MODES, planes, rows, width), F32),
            jax.ShapeDtypeStruct((count, MODES), F32),
        ),
        in_specs=[vmem, vmem, vmem, smem, any_space],
        out_specs=(any_space, vmem),
        scratch_shapes=[
            pltpu.VMEM(filt_shape, BF16),
            pltpu.VMEM((planes, chunks, MODES, ROWS, width), F32),
            pltpu.VMEM((MODES, MODES, 128), F32),
            pltpu.VMEM((MODES, 128), F32),
            dma((planes, chunks)),
            dma((planes, chunks)),
        ],
        compiler_params=pltpu.CompilerParams(vmem_limit_bytes=60 * 2**20),
    )(packed, energies[None, :], energies[:, None], plane_weight, filt)
    return modes, basis


def solution(mesh):
    torus = Mesh(mesh.devices.reshape(4, 4, 2, 2, mesh.shape["gy"]), NAMES)
    in_specs = (P(None, GZ, "gy", None), P(), P(GZ))
    out_specs = (P(None, GZ, "gy", None), P())
    return jax.shard_map(local, mesh=torus, in_specs=in_specs, out_specs=out_specs, check_vma=False)
```

time: 243 us -> 109 us (0.45)
  Pallas kernels: 0 us -> 106 us
  blocking collectives: 86.6 us -> 0 us
  matrix products: 53.4 us -> 0 us
  other arithmetic: 49.7 us -> 0 us
  waiting for transfers between devices: 35.1 us -> 0 us
  starting transfers between devices: 8.22 us -> 0 us
  local copies, waits for them, and re-layouts: 8.63 us -> 2.75 us
    pallas_call x0 -> x2, Pallas kernels: none -> 106 us  [the longest x1 90.2 us: local(): pl.pallas_call(functools.partial(gram_kernel, chunks), name='gram', out_s...]
    psum x5 -> x0, blocking collectives: 86.6 us -> none  [one_axis_at_a_time(): return functools.reduce(lax.psum, axes, x)]
    dot_general x15 -> x0, matrix products: 52.1 us -> none  [the longest x1 32.1 us: local(): jnp.dot(weighted, flat.T, precision=lax.Precision.HIGHEST) / total]
    ppermute x2 -> x0, waiting for transfers between devices: 35.1 us -> none  [the longest x1 35.1 us: padded_2(): lax.ppermute(lax.slice_in_dim(block, block.shape[dim] - width, None, axis...]
    mul x2 -> x0, other arithmetic: 25.5 us -> none  [the longest x1 13.5 us: local(): weighted = (filtered * plane_weight[None, :, None, None]).reshape(count, -1)]
    another operation x30 -> x0, other arithmetic: 24.1 us -> none  [the longest x18 12.9 us: local(): jnp.linalg.cholesky(jnp.dot(image.T, image, precision=lax.Precision.HIGHE...]
    ppermute x2 -> x0, starting transfers between devices: 8.22 us -> none  [the longest x1 8.14 us: padded_2(): lax.ppermute(lax.slice_in_dim(block, 0, width, axis=dim), axis, backward)]
    unnamed x7 -> x0, local copies, waits for them, and re-layouts: 4.45 us -> none
  transfers between devices with their start and end apart: 2 -> 0, of which waited for: 1 -> 0; matrix products, arithmetic and copies ran while one was open for 0% -> 0% of each run, Pallas kernels for 0% -> 0%
where the time goes in v1:
time: 109 us
  Pallas kernels  106 us (97%)
  local copies, waits for them, and re-layouts  2.75 us (3%)
    pallas_call x1, Pallas kernels, local(): pl.pallas_call(functools.partial(gram_kernel, chunks), name='gram', out_s...  90.2 us
    pallas_call x1, Pallas kernels, local(): pl.pallas_call(functools.partial(mode_kernel, chunks, cells), name='modes...  15.7 us

profile of v1, /device:TPU:0, one launch (start us, length us, event | category | flops | bytes accessed | tf_op | source)
XLA Modules:
  0.0 109.2 jit_solution(1642355260613170930)
XLA Ops:
  0.6 1.3 %copy.5.energy_col = f32[48,1]{1,0:T(8,128)} copy(f32[48,1]{0,1:T(1,128)} %bitcast.2) | data formatting | bytes 384 | tf_op jit(solution)/shard_map/broadcast_in_dim | solution.py:411
  2.0 90.2 %gram.1 = (bf16[4,8,768,256]{3,2,1,0:T(8,128)(2,1)}, f32[24,128]{1,0:T(8,128)}) custom-call(f32[48,4,64,256]{3,2,1,0:T(8,128)} %snap.1, f32[4]{0:T(128)} %weight.3), custom_call_target="tpu_custom_call" | custom-call | tf_op jit(solution)/shard_map/gram/pallas_call | solution.py:360
  92.2 15.7 %modes.1 = (f32[16,4,64,256]{3,2,1,0:T(8,128)}, f32[48,16]{1,0:T(8,128)}) custom-call(f32[24,128]{1,0:T(8,128)} %get-tuple-element.4.packed, f32[1,48]{1,0:T(1,128)} %bitcast.3, f32[48,1]{1,0:T(8,128)} %copy.5.energy_col, f32[4]{0:T(128)} %weight.3, bf16[4,8,768,256]{3,2,1,0:T(8,128)(2,1)} %get-tuple-element.5.filt_in), custom_call_target="tpu_custom_call" | custom-call | tf_op jit(solution)/shard_map/modes/pallas_call | solution.py:393
  107.8 1.4 %copy.6 = f32[48,16]{0,1:T(8,128)} copy(f32[48,16]{1,0:T(8,128)} %get-tuple-element.7) | data formatting | bytes 6144 | tf_op jit(solution)/shard_map/modes/pallas_call | solution.py:393

commit v2 on v1

--- a/solution.py
+++ b/solution.py
@@ -17,6 +17,9 @@
 F32 = jnp.float32
 BF16 = jnp.bfloat16
 ROWS = 8
+GROUP = 4
+VMEM_GRAM = 40 * 2**20
+VMEM_MODES = 24 * 2**20
 
 
 def nt(a, b, precision=None):
@@ -51,19 +54,17 @@
     chunks,
     snap,
     weight,
-    filt_out,
+    filt,
     gram_out,
     field,
-    below,
-    above,
-    filt,
+    halos,
     total,
+    choose,
     weights,
     line_buf,
     plane_buf,
     load_sem,
     small_sem,
-    store_sem,
     halo_send,
     halo_recv,
     line_send,
@@ -101,16 +102,21 @@
         rows = pl.ds(pl.multiple_of(chunk * ROWS, ROWS), ROWS)
         return pltpu.make_async_remote_copy(
             src_ref=snap.at[:, 3 if side == 0 else 0, rows, :],
-            dst_ref=(below if side == 0 else above).at[chunk],
+            dst_ref=halos.at[side, chunk],
             send_sem=halo_send.at[side, chunk],
             recv_sem=halo_recv.at[side, chunk],
             device_id=upper if side == 0 else lower,
             device_id_type=MESH,
         )
 
-    def store(chunk, z):
-        return pltpu.make_async_copy(
-            filt.at[z, chunk], filt_out.at[z, chunk], store_sem.at[chunk, z]
+    def arrival(chunk, side):
+        return pltpu.make_async_remote_copy(
+            src_ref=halos.at[side, chunk],
+            dst_ref=halos.at[side, chunk],
+            send_sem=halo_send.at[side, chunk],
+            recv_sem=halo_recv.at[side, chunk],
+            device_id=upper,
+            device_id_type=MESH,
         )
 
     pl.semaphore_wait(barrier, 24)
@@ -123,12 +129,16 @@
         for z in range(4):
             load(chunk, z).start()
     read.wait()
-    root = [jnp.sqrt(jnp.full((1, 256), weights[z], F32)) for z in range(4)]
     total[...] = jnp.zeros_like(total)
+    place = lax.broadcasted_iota(jnp.int32, (2 * tall, 128), 0) // ROWS
+    place = jnp.where(place < count, place, place - count + 64)
+    choose[...] = (
+        (place == lax.broadcasted_iota(jnp.int32, (2 * tall, 128), 1)).astype(F32).astype(BF16)
+    )
 
     def smooth(a, b, c, z):
-        value = (0.25 * root[z]) * (a + c) + (0.5 * root[z]) * b
-        return value
+        root = jnp.sqrt(jnp.full((1, 256), weights[z], F32))
+        return (0.25 * root) * (a + c) + (0.5 * root) * b
 
     def accumulate(chunk, planes, values):
         highs, lows = [], []
@@ -140,10 +150,7 @@
             lows.append(low)
         high = jnp.concatenate(highs, axis=1)
         low = jnp.concatenate(lows, axis=1)
-        total[:, :tall] += nt(high, high)
-        total[:, tall:] += nt(high, low)
-        for z in planes:
-            store(chunk, z).start()
+        total[...] += nt(high, jnp.concatenate([high, low], axis=0))
 
     def flat(ref):
         return ref[...].reshape(tall, ref.shape[-1])
@@ -159,19 +166,21 @@
 
     lax.fori_loop(0, chunks, inner, 0)
 
-    def outer(chunk, carry):
-        for side in range(2):
-            halo(chunk, side).wait_recv()
-        first = smooth(
-            flat(below.at[chunk]), flat(field.at[chunk, 0]), flat(field.at[chunk, 1]), 0
-        )
-        last = smooth(
-            flat(field.at[chunk, 2]), flat(field.at[chunk, 3]), flat(above.at[chunk]), 3
-        )
-        accumulate(chunk, (0, 3), [first, last])
-        return carry
-
-    lax.fori_loop(0, chunks, outer, 0)
+    for side in (1 - c, c * 1):
+        z = side * 3
+
+        def outer(chunk, carry, side=side, z=z):
+            arrival(chunk, side).wait_recv()
+            value = smooth(
+                flat(halos.at[side, chunk]),
+                flat(field.at[chunk, z]),
+                flat(field.at[chunk, 1 + side]),
+                z,
+            )
+            accumulate(chunk, (z,), [value])
+            return carry
+
+        lax.fori_loop(0, chunks, outer, 0)
 
     whole = total[:, :tall] + 2.0 * total[:, tall:]
     keep = lax.broadcasted_iota(jnp.int32, (tall, tall), 0) % ROWS == (
@@ -180,10 +189,12 @@
     picked = jnp.sum(jnp.where(keep, whole, 0.0).reshape(count, ROWS, tall), axis=1)
     half = count // 2
     wide = jnp.concatenate([picked[:half], picked[half:]], axis=1)
-    place = lax.broadcasted_iota(jnp.int32, (128, 2 * tall), 1) // ROWS
-    place = jnp.where(place < count, place, place - count + 64)
-    choose = (place == lax.broadcasted_iota(jnp.int32, (128, 2 * tall), 0)).astype(F32)
-    packed = nt(wide, choose, HIGH)
+    packed = jnp.zeros((half, 128), F32)
+    rest = wide
+    for part in range(3):
+        piece = rest.astype(BF16)
+        rest = rest - piece.astype(F32)
+        packed += jnp.dot(piece, choose[...], preferred_element_type=F32)
 
     def reduce(value, buf, me, size, device_of, send, recv):
         buf[me] = value
@@ -229,8 +240,6 @@
     for chunk in range(chunks):
         for side in range(2):
             halo(chunk, side).wait_send()
-        for z in range(4):
-            store(chunk, z).wait()
 
 
 def mode_kernel(
@@ -238,41 +247,29 @@
     cells,
     packed,
     energy_row,
-    energy_col,
     weight,
-    filt_in,
+    filt,
     modes_out,
     basis_out,
-    filt,
     modes,
     columns,
     lines,
-    load_sem,
     store_sem,
 ):
     count = energy_row.shape[1]
     tall = count * ROWS
 
-    def load(chunk, z):
-        return pltpu.make_async_copy(
-            filt_in.at[z, chunk], filt.at[z, chunk], load_sem.at[z, chunk]
-        )
-
     def store(chunk, z):
         rows = pl.ds(pl.multiple_of(chunk * ROWS, ROWS), ROWS)
         return pltpu.make_async_copy(
             modes.at[z, chunk], modes_out.at[:, z, rows, :], store_sem.at[z, chunk]
         )
 
-    for z in range(4):
-        for chunk in range(chunks):
-            load(chunk, z).start()
-
     half = count // 2
     value = packed[...]
     gram = jnp.concatenate([value[:, :count], value[:, 64 : 64 + count]], axis=0)
-    gram = 0.5 * (gram + gram.T)
-    gram = gram * (energy_col[...] * energy_row[...]) / cells
+    gram = (gram * energy_row[...]).T * energy_row[...]
+    gram = (0.5 / cells) * (gram + gram.T)
 
     eye = (
         lax.broadcasted_iota(jnp.int32, (MODES, count), 0)
@@ -292,7 +289,6 @@
         for k in range(MODES):
             scale = lax.rsqrt(entry[k, k])
             inverse = scale * scale
-            row[k] = row[k]
             factors = {i: entry[i, k] * inverse for i in range(k + 1, MODES)}
             for i in range(k + 1, MODES):
                 row[i] = row[i] - factors[i] * row[k]
@@ -305,7 +301,7 @@
 
     lines[...] = jnp.zeros_like(lines)
     basis = lax.fori_loop(0, ITERS, iterate, eye)
-    basis_out[...] = basis.T
+    basis_out[...] = basis
     projected = jnp.dot(basis, gram, precision=HIGH, preferred_element_type=F32)
     norms = jnp.sum(basis * projected, axis=1, keepdims=True)
     scaled = basis * energy_row[...] * lax.rsqrt(norms)
@@ -314,35 +310,35 @@
     spread = (
         lax.broadcasted_iota(jnp.int32, (count, tall), 0)
         == lax.broadcasted_iota(jnp.int32, (count, tall), 1) // ROWS
-    ).astype(BF16)
-    both = jnp.dot(both, spread, preferred_element_type=F32).astype(BF16)
-    tallest = 2 * MODES * ROWS
-    repeat = (
-        lax.broadcasted_iota(jnp.int32, (tallest, 2 * MODES), 0) // ROWS
-        == lax.broadcasted_iota(jnp.int32, (tallest, 2 * MODES), 1)
-    ).astype(BF16)
-    both = jnp.dot(repeat, both, preferred_element_type=F32)
-    keep = lax.broadcasted_iota(jnp.int32, (tallest, tall), 0) % ROWS == (
-        lax.broadcasted_iota(jnp.int32, (tallest, tall), 1) % ROWS
-    )
-    both = jnp.where(keep, both, 0.0).astype(BF16)
+    ).astype(F32).astype(BF16)
+    both = jnp.dot(both, spread, preferred_element_type=F32)
+    both = jnp.broadcast_to(both[:, None, :], (2 * MODES, ROWS, tall))
+    keep = lax.broadcasted_iota(jnp.int32, both.shape, 1) == (
+        lax.broadcasted_iota(jnp.int32, both.shape, 2) % ROWS
+    )
+    both = jnp.where(keep, both, 0.0).reshape(2 * MODES * ROWS, tall).astype(BF16)
     top, bottom = both[: MODES * ROWS], both[MODES * ROWS :]
-
-    for z in range(4):
-        back = lax.rsqrt(jnp.full((1, 256), weight[z], F32))
-
-        def project(chunk, carry, z=z, back=back):
-            load(chunk, z).wait()
-            high = filt[z, chunk, :tall, :]
-            low = filt[z, chunk, tall:, :]
-            raw = jnp.dot(top, high, preferred_element_type=F32)
-            raw += jnp.dot(top, low, preferred_element_type=F32)
-            raw += jnp.dot(bottom, high, preferred_element_type=F32)
-            modes[z, chunk] = (raw * back).reshape(MODES, ROWS, raw.shape[-1])
-            store(chunk, z).start()
-            return carry
-
-        lax.fori_loop(0, chunks, project, 0)
+    matrix = jnp.concatenate([top, top, bottom], axis=1)
+
+    def project(step, carry):
+        z = step // (chunks // GROUP)
+        first = lax.rem(step, chunks // GROUP) * GROUP
+        back = lax.rsqrt(jnp.full((1, modes.shape[-1]), weight[z], F32))
+        fields = []
+        for i in range(GROUP):
+            value = filt[z, first + i]
+            fields.append(jnp.concatenate([value, value[:tall]], axis=0))
+        raw = jnp.dot(
+            matrix, jnp.concatenate(fields, axis=1), preferred_element_type=F32
+        )
+        width = modes.shape[-1]
+        for i in range(GROUP):
+            part = raw[:, i * width : (i + 1) * width] * back
+            modes[z, first + i] = part.reshape(MODES, ROWS, width)
+            store(first + i, z).start()
+        return carry
+
+    lax.fori_loop(0, 4 * chunks // GROUP, project, 0)
     for z in range(4):
         for chunk in range(chunks):
             store(chunk, z).wait()
@@ -353,6 +349,7 @@
     chunks = rows // ROWS
     tall = count * ROWS
     any_space = pl.BlockSpec(memory_space=pl.ANY)
+    hbm = pl.BlockSpec(memory_space=pltpu.HBM)
     vmem = pl.BlockSpec(memory_space=pltpu.VMEM)
     smem = pl.BlockSpec(memory_space=pltpu.SMEM)
     dma = pltpu.SemaphoreType.DMA
@@ -361,23 +358,21 @@
         functools.partial(gram_kernel, chunks),
         name="gram",
         out_shape=(
-            jax.ShapeDtypeStruct(filt_shape, BF16),
-            jax.ShapeDtypeStruct((count // 2, 128), F32),
+            pltpu.VMEM(filt_shape, BF16),
+            pltpu.VMEM((count // 2, 128), F32),
         ),
-        in_specs=[any_space, any_space],
-        out_specs=(any_space, vmem),
+        in_specs=[hbm, hbm],
+        out_specs=(vmem, vmem),
         scratch_shapes=[
             pltpu.VMEM((chunks, planes, count, ROWS, width), F32),
-            pltpu.VMEM((chunks, count, ROWS, width), F32),
-            pltpu.VMEM((chunks, count, ROWS, width), F32),
-            pltpu.VMEM(filt_shape, BF16),
+            pltpu.VMEM((2, chunks, count, ROWS, width), F32),
             pltpu.VMEM((tall, 2 * tall), F32),
+            pltpu.VMEM((2 * tall, 128), BF16),
             pltpu.SMEM((planes,), F32),
             pltpu.VMEM((8, count // 2, 128), F32),
             pltpu.VMEM((16, count // 2, 128), F32),
             dma((chunks, planes)),
             dma,
-            dma((chunks, planes)),
             dma((2, chunks)),
             dma((2, chunks)),
             dma((8,)),
@@ -386,30 +381,36 @@
             dma((16,)),
         ],
         compiler_params=pltpu.CompilerParams(
-            collective_id=0, has_side_effects=True, vmem_limit_bytes=60 * 2**20
+            collective_id=0, has_side_effects=True, vmem_limit_bytes=VMEM_GRAM
         ),
-    )(snapshots, plane_weight)
+    )(
+        pltpu.with_memory_space_constraint(snapshots, pltpu.HBM),
+        pltpu.with_memory_space_constraint(plane_weight, pltpu.HBM),
+    )
     cells = planes * 64 * rows * 2 * width
     modes, basis = pl.pallas_call(
         functools.partial(mode_kernel, chunks, cells),
         name="modes",
         out_shape=(
             jax.ShapeDtypeStruct((MODES, planes, rows, width), F32),
-            jax.ShapeDtypeStruct((count, MODES), F32),
+            jax.ShapeDtypeStruct((MODES, count), F32),
         ),
-        in_specs=[vmem, vmem, vmem, smem, any_space],
+        in_specs=[vmem, vmem, smem, vmem],
         out_specs=(any_space, vmem),
         scratch_shapes=[
-            pltpu.VMEM(filt_shape, BF16),
             pltpu.VMEM((planes, chunks, MODES, ROWS, width), F32),
             pltpu.VMEM((MODES, MODES, 128), F32),
             pltpu.VMEM((MODES, 128), F32),
             dma((planes, chunks)),
-            dma((planes, chunks)),
         ],
-        compiler_params=pltpu.CompilerParams(vmem_limit_bytes=60 * 2**20),
-    )(packed, energies[None, :], energies[:, None], plane_weight, filt)
-    return modes, basis
+        compiler_params=pltpu.CompilerParams(vmem_limit_bytes=VMEM_MODES),
+    )(
+        pltpu.with_memory_space_constraint(packed, pltpu.VMEM),
+        energies[None, :],
+        plane_weight,
+        pltpu.with_memory_space_constraint(filt, pltpu.VMEM),
+    )
+    return modes, basis.T
 
 
 def solution(mesh):

time: 109 us -> 101 us (0.927)
  Pallas kernels: 106 us -> 100 us
  local copies, waits for them, and re-layouts: 2.75 us -> 0.01 us
    pallas_call x1, Pallas kernels: 15.7 us -> 10.9 us  [local(): pl.pallas_call(functools.partial(mode_kernel, chunks, cells), name='modes...]
    pallas_call x1 -> x0, local copies, waits for them, and re-layouts: 1.41 us -> none  [local(): pl.pallas_call(functools.partial(mode_kernel, chunks, cells), name='modes...]
    broadcast_in_dim x1 -> x0, local copies, waits for them, and re-layouts: 1.34 us -> none  [local(): energies[:, None]]
    pallas_call x1, Pallas kernels: 90.2 us -> 89.1 us  [local(): pl.pallas_call(functools.partial(gram_kernel, chunks), name='gram', out_s...]
where the time goes in v2:
time: 101 us
  Pallas kernels  100 us (99%)
    pallas_call x1, Pallas kernels, local(): pl.pallas_call(functools.partial(gram_kernel, chunks), name='gram', out_s...  89.1 us
    pallas_call x1, Pallas kernels, local(): pl.pallas_call(functools.partial(mode_kernel, chunks, cells), name='modes...  10.9 us

profile of v2, /device:TPU:0, one launch (start us, length us, event | category | flops | bytes accessed | tf_op | source)
XLA Modules:
  0.0 100.6 jit_solution(1503088976095878186)
XLA Ops:
  0.6 0.0 copy-start
  0.6 0.0 copy-start.1
  0.6 89.1 %gram.1 = (bf16[4,8,768,256]{3,2,1,0:T(8,128)(2,1)S(1)}, f32[24,128]{1,0:T(8,128)S(1)}) custom-call(f32[48,4,64,256]{3,2,1,0:T(8,128)} %snap.1, f32[4]{0:T(128)} %weight.3), custom_call_target="tpu_custom_call" | custom-call | tf_op jit(solution)/shard_map/gram/pallas_call | solution.py:357
  89.7 0.0 copy-done
  89.7 0.0 copy-done.1
  89.8 10.9 %modes.1 = (f32[16,4,64,256]{3,2,1,0:T(8,128)}, f32[16,48]{1,0:T(8,128)}) custom-call(f32[24,128]{1,0:T(8,128)S(1)} %get-tuple-element.6.packed, f32[1,48]{1,0:T(1,128)S(1)} %bitcast.2, f32[4]{0:T(128)S(1)} %copy-done, bf16[4,8,768,256]{3,2,1,0:T(8,128)(2,1)S(1)} %get-tuple-element.7.filt), custom_call_target="tpu_custom_call" | custom-call | tf_op jit(solution)/shard_map/modes/pallas_call | solution.py:391
Async XLA Ops:
  0.6 89.1 %copy-start = (f32[4]{0:T(128)S(1)}, f32[4]{0:T(128)}, u32[]{:S(2)}) copy-start(f32[4]{0:T(128)} %weight.3) | copy-start | bytes 52
  0.6 89.1 %copy-start.1 = (f32[48]{0:T(128)S(1)}, f32[48]{0:T(128)}, u32[]{:S(2)}) copy-start(f32[48]{0:T(128)} %param.4) | copy-start | bytes 580

commit v3 on v2

--- a/solution.py
+++ b/solution.py
@@ -52,19 +52,24 @@
 
 def gram_kernel(
     chunks,
+    cells,
     snap,
     weight,
+    energy_in,
     filt,
     gram_out,
     field,
     halos,
     total,
     choose,
+    levels,
+    energy_row,
     weights,
     line_buf,
     plane_buf,
     load_sem,
     small_sem,
+    energy_sem,
     halo_send,
     halo_recv,
     line_send,
@@ -125,16 +130,27 @@
             halo(chunk, side).start()
     read = pltpu.make_async_copy(weight, weights, small_sem)
     read.start()
+    fetch = pltpu.make_async_copy(energy_in, energy_row, energy_sem)
+    fetch.start()
     for chunk in range(chunks):
         for z in range(4):
             load(chunk, z).start()
     read.wait()
+    fetch.wait()
     total[...] = jnp.zeros_like(total)
     place = lax.broadcasted_iota(jnp.int32, (2 * tall, 128), 0) // ROWS
     place = jnp.where(place < count, place, place - count + 64)
     choose[...] = (
         (place == lax.broadcasted_iota(jnp.int32, (2 * tall, 128), 1)).astype(F32).astype(BF16)
     )
+
+    half = count // 2
+    pad = jnp.zeros((1, 64 - count), F32)
+    energy = energy_row[...]
+    across = jnp.concatenate([energy, pad, energy, pad], axis=1)
+    down = jnp.broadcast_to(energy, (128, count)).T
+    lane = lax.broadcasted_iota(jnp.int32, (half, 128), 1)
+    levels[...] = jnp.where(lane < 64, down[:half], down[half:]) * across * (0.5 / cells)
 
     def smooth(a, b, c, z):
         root = jnp.sqrt(jnp.full((1, 256), weights[z], F32))
@@ -187,7 +203,6 @@
         lax.broadcasted_iota(jnp.int32, (tall, tall), 1) % ROWS
     )
     picked = jnp.sum(jnp.where(keep, whole, 0.0).reshape(count, ROWS, tall), axis=1)
-    half = count // 2
     wide = jnp.concatenate([picked[:half], picked[half:]], axis=1)
     packed = jnp.zeros((half, 128), F32)
     rest = wide
@@ -234,7 +249,7 @@
     packed, plane_copies = reduce(
         packed, plane_buf, plane, 16, plane_device, plane_send, plane_recv
     )
-    gram_out[...] = packed
+    gram_out[...] = packed * levels[...]
     for copy in line_copies + plane_copies:
         copy.wait_send()
     for chunk in range(chunks):
@@ -244,7 +259,6 @@
 
 def mode_kernel(
     chunks,
-    cells,
     packed,
     energy_row,
     weight,
@@ -254,6 +268,7 @@
     modes,
     columns,
     lines,
+    square_gram,
     store_sem,
 ):
     count = energy_row.shape[1]
@@ -265,44 +280,50 @@
             modes.at[z, chunk], modes_out.at[:, z, rows, :], store_sem.at[z, chunk]
         )
 
-    half = count // 2
+    square_gram[...] = jnp.zeros_like(square_gram)
     value = packed[...]
     gram = jnp.concatenate([value[:, :count], value[:, 64 : 64 + count]], axis=0)
-    gram = (gram * energy_row[...]).T * energy_row[...]
-    gram = (0.5 / cells) * (gram + gram.T)
-
-    eye = (
-        lax.broadcasted_iota(jnp.int32, (MODES, count), 0)
-        == lax.broadcasted_iota(jnp.int32, (MODES, count), 1)
-    ).astype(F32)
-
-    def iterate(step, basis):
-        image = jnp.dot(basis, gram, precision=HIGH, preferred_element_type=F32)
+    square_gram[:count, :count] = gram + gram.T
+    gram = square_gram[...]
+
+    def eliminate(image, *arrays):
         square = nt(image, image, HIGH)
         for j in range(MODES):
             columns[j] = jnp.broadcast_to(square[:, j : j + 1], (MODES, 128))
-        lines[:, :count] = image
+        for i, array in enumerate(arrays):
+            lines[i] = array
         entry = {
             (i, j): columns[j, i : i + 1, :] for j in range(MODES) for i in range(j, MODES)
         }
-        row = [lines[i : i + 1, :] for i in range(MODES)]
+        rows = [[lines[n, i : i + 1, :] for i in range(MODES)] for n in range(len(arrays))]
         for k in range(MODES):
+            inverse = 1.0 / entry[k, k]
+            if k + 1 < MODES:
+                side = entry[k + 1, k]
+                entry[k + 1, k + 1] = entry[k + 1, k + 1] - (side * side) * inverse
+            for i in range(k + 1, MODES):
+                factor = entry[i, k] * inverse
+                for row in rows:
+                    row[i] = row[i] - factor * row[k]
+                for j in range(k + 1, i + 1):
+                    if (i, j) != (k + 1, k + 1):
+                        entry[i, j] = entry[i, j] - factor * entry[j, k]
             scale = lax.rsqrt(entry[k, k])
-            inverse = scale * scale
-            factors = {i: entry[i, k] * inverse for i in range(k + 1, MODES)}
-            for i in range(k + 1, MODES):
-                row[i] = row[i] - factors[i] * row[k]
-                for j in range(k + 1, i + 1):
-                    entry[i, j] = entry[i, j] - factors[i] * entry[j, k]
-            row[k] = row[k] * scale
-        for i in range(MODES):
-            lines[i : i + 1, :] = row[i]
-        return lines[:, :count]
-
-    lines[...] = jnp.zeros_like(lines)
-    basis = lax.fori_loop(0, ITERS, iterate, eye)
+            for row in rows:
+                row[k] = row[k] * scale
+        for n, row in enumerate(rows):
+            for i in range(MODES):
+                lines[n, i : i + 1, :] = row[i]
+        return [lines[n] for n in range(len(arrays))]
+
+    def apply(image):
+        return jnp.dot(image, gram, precision=HIGH, preferred_element_type=F32)
+
+    image = lax.fori_loop(
+        0, ITERS - 1, lambda step, image: eliminate(image, apply(image))[0], gram[:MODES]
+    )
+    basis, projected = (x[:, :count] for x in eliminate(image, image, apply(image)))
     basis_out[...] = basis
-    projected = jnp.dot(basis, gram, precision=HIGH, preferred_element_type=F32)
     norms = jnp.sum(basis * projected, axis=1, keepdims=True)
     scaled = basis * energy_row[...] * lax.rsqrt(norms)
     high, low = split(scaled)
@@ -322,7 +343,7 @@
 
     def project(step, carry):
         z = step // (chunks // GROUP)
-        first = lax.rem(step, chunks // GROUP) * GROUP
+        first = (step % (chunks // GROUP)) * GROUP
         back = lax.rsqrt(jnp.full((1, modes.shape[-1]), weight[z], F32))
         fields = []
         for i in range(GROUP):
@@ -338,7 +359,8 @@
             store(first + i, z).start()
         return carry
 
-    lax.fori_loop(0, 4 * chunks // GROUP, project, 0)
+    for step in range(4 * chunks // GROUP):
+        project(step, 0)
     for z in range(4):
         for chunk in range(chunks):
             store(chunk, z).wait()
@@ -347,6 +369,7 @@
 def local(snapshots, energies, plane_weight):
     count, planes, rows, width = snapshots.shape
     chunks = rows // ROWS
+    cells = planes * 64 * rows * 2 * width
     tall = count * ROWS
     any_space = pl.BlockSpec(memory_space=pl.ANY)
     hbm = pl.BlockSpec(memory_space=pltpu.HBM)
@@ -355,23 +378,26 @@
     dma = pltpu.SemaphoreType.DMA
     filt_shape = (planes, chunks, 2 * tall, width)
     filt, packed = pl.pallas_call(
-        functools.partial(gram_kernel, chunks),
+        functools.partial(gram_kernel, chunks, cells),
         name="gram",
         out_shape=(
             pltpu.VMEM(filt_shape, BF16),
             pltpu.VMEM((count // 2, 128), F32),
         ),
-        in_specs=[hbm, hbm],
+        in_specs=[hbm, hbm, hbm],
         out_specs=(vmem, vmem),
         scratch_shapes=[
             pltpu.VMEM((chunks, planes, count, ROWS, width), F32),
             pltpu.VMEM((2, chunks, count, ROWS, width), F32),
             pltpu.VMEM((tall, 2 * tall), F32),
             pltpu.VMEM((2 * tall, 128), BF16),
+            pltpu.VMEM((count // 2, 128), F32),
+            pltpu.VMEM((1, count), F32),
             pltpu.SMEM((planes,), F32),
             pltpu.VMEM((8, count // 2, 128), F32),
             pltpu.VMEM((16, count // 2, 128), F32),
             dma((chunks, planes)),
+            dma,
             dma,
             dma((2, chunks)),
             dma((2, chunks)),
@@ -386,10 +412,10 @@
     )(
         pltpu.with_memory_space_constraint(snapshots, pltpu.HBM),
         pltpu.with_memory_space_constraint(plane_weight, pltpu.HBM),
-    )
-    cells = planes * 64 * rows * 2 * width
+        pltpu.with_memory_space_constraint(energies[None, :], pltpu.HBM),
+    )
     modes, basis = pl.pallas_call(
-        functools.partial(mode_kernel, chunks, cells),
+        functools.partial(mode_kernel, chunks),
         name="modes",
         out_shape=(
             jax.ShapeDtypeStruct((MODES, planes, rows, width), F32),
@@ -400,7 +426,8 @@
         scratch_shapes=[
             pltpu.VMEM((planes, chunks, MODES, ROWS, width), F32),
             pltpu.VMEM((MODES, MODES, 128), F32),
-            pltpu.VMEM((MODES, 128), F32),
+            pltpu.VMEM((2, MODES, 128), F32),
+            pltpu.VMEM((128, 128), F32),
             dma((planes, chunks)),
         ],
         compiler_params=pltpu.CompilerParams(vmem_limit_bytes=VMEM_MODES),

time: 101 us -> 98.5 us (0.975)
  Pallas kernels: 100 us -> 97.7 us
    pallas_call x2, Pallas kernels: 100 us -> 97.7 us  [the longest x1 89.1 us: local(): pl.pallas_call(functools.partial(gram_kernel, chunks, cells), name='gram'...]
where the time goes in v3:
time: 98.5 us; the launch traced here: 98.4 us
  Pallas kernels  97.7 us (99%)
    pallas_call x1, Pallas kernels, local(): pl.pallas_call(functools.partial(gram_kernel, chunks, cells), name='gram'...  89.1 us
    pallas_call x1, Pallas kernels, local(): pl.pallas_call(functools.partial(mode_kernel, chunks), name='modes', out_...  8.64 us

profile of v3, /device:TPU:0, one launch (start us, length us, event | category | flops | bytes accessed | tf_op | source)
XLA Modules:
  0.0 98.4 jit_solution(5214452230650107186)
XLA Ops:
  0.6 0.0 copy-start
  0.6 0.0 copy-start.1
  0.6 89.1 %gram.1 = (bf16[4,8,768,256]{3,2,1,0:T(8,128)(2,1)S(1)}, f32[24,128]{1,0:T(8,128)S(1)}) custom-call(f32[48,4,64,256]{3,2,1,0:T(8,128)} %snap.1, f32[4]{0:T(128)} %weight.3, f32[1,48]{1,0:T(1,128)} %bitcast.2), custom_call_target="tpu_custom_call" | custom-call | tf_op jit(solution)/shard_map/gram/pallas_call | solution.py:380
  89.7 0.0 copy-done
  89.8 0.0 copy-done.1
  89.8 8.6 %modes.1 = (f32[16,4,64,256]{3,2,1,0:T(8,128)}, f32[16,48]{1,0:T(8,128)}) custom-call(f32[24,128]{1,0:T(8,128)S(1)} %get-tuple-element.6.packed, f32[1,48]{1,0:T(1,128)S(1)} %bitcast.3, f32[4]{0:T(128)S(1)} %copy-done, bf16[4,8,768,256]{3,2,1,0:T(8,128)(2,1)S(1)} %get-tuple-element.7.filt), custom_call_target="tpu_custom_call" | custom-call | tf_op jit(solution)/shard_map/modes/pallas_call | solution.py:417
Async XLA Ops:
  0.6 89.1 %copy-start = (f32[4]{0:T(128)S(1)}, f32[4]{0:T(128)}, u32[]{:S(2)}) copy-start(f32[4]{0:T(128)} %weight.3) | copy-start | bytes 52
  0.6 89.1 %copy-start.1 = (f32[48]{0:T(128)S(1)}, f32[48]{0:T(128)}, u32[]{:S(2)}) copy-start(f32[48]{0:T(128)} %param.4) | copy-start | bytes 580

commit v4 on v3

--- a/solution.py
+++ b/solution.py
@@ -17,6 +17,7 @@
 F32 = jnp.float32
 BF16 = jnp.bfloat16
 ROWS = 8
+BLOCK = 16
 GROUP = 4
 VMEM_GRAM = 40 * 2**20
 VMEM_MODES = 24 * 2**20
@@ -104,9 +105,8 @@
         )
 
     def halo(chunk, side):
-        rows = pl.ds(pl.multiple_of(chunk * ROWS, ROWS), ROWS)
         return pltpu.make_async_remote_copy(
-            src_ref=snap.at[:, 3 if side == 0 else 0, rows, :],
+            src_ref=field.at[chunk, 3 if side == 0 else 0],
             dst_ref=halos.at[side, chunk],
             send_sem=halo_send.at[side, chunk],
             recv_sem=halo_recv.at[side, chunk],
@@ -124,33 +124,45 @@
             device_id_type=MESH,
         )
 
-    pl.semaphore_wait(barrier, 24)
     for chunk in range(chunks):
-        for side in range(2):
-            halo(chunk, side).start()
+        for z in (3, 0):
+            load(chunk, z).start()
+    for chunk in range(chunks):
+        for z in (1, 2):
+            load(chunk, z).start()
     read = pltpu.make_async_copy(weight, weights, small_sem)
     read.start()
     fetch = pltpu.make_async_copy(energy_in, energy_row, energy_sem)
     fetch.start()
+    pl.semaphore_wait(barrier, 24)
     for chunk in range(chunks):
-        for z in range(4):
-            load(chunk, z).start()
+        for side in range(2):
+            load(chunk, 3 if side == 0 else 0).wait()
+            halo(chunk, side).start()
     read.wait()
     fetch.wait()
     total[...] = jnp.zeros_like(total)
-    place = lax.broadcasted_iota(jnp.int32, (2 * tall, 128), 0) // ROWS
-    place = jnp.where(place < count, place, place - count + 64)
-    choose[...] = (
-        (place == lax.broadcasted_iota(jnp.int32, (2 * tall, 128), 1)).astype(F32).astype(BF16)
-    )
-
-    half = count // 2
-    pad = jnp.zeros((1, 64 - count), F32)
+    place = lax.broadcasted_iota(jnp.int32, (3 * tall, 128), 0) // ROWS
+    lane = lax.broadcasted_iota(jnp.int32, (3 * tall, 128), 1)
+    second, third = place - count, place - 2 * count
+    second = jnp.where(second >= BLOCK, second + 2 * BLOCK, -1)
+    third = jnp.where(third >= 2 * BLOCK, third + 3 * BLOCK, -1)
+    target = jnp.where(place < count, place, jnp.where(place < 2 * count, second, third))
+    choose[...] = (target == lane).astype(F32).astype(BF16)
+
     energy = energy_row[...]
-    across = jnp.concatenate([energy, pad, energy, pad], axis=1)
+    across = jnp.concatenate(
+        [energy, energy[:, BLOCK:], energy[:, 2 * BLOCK :], jnp.zeros((1, 2 * BLOCK), F32)],
+        axis=1,
+    )
     down = jnp.broadcast_to(energy, (128, count)).T
-    lane = lax.broadcasted_iota(jnp.int32, (half, 128), 1)
-    levels[...] = jnp.where(lane < 64, down[:half], down[half:]) * across * (0.5 / cells)
+    lane = lax.broadcasted_iota(jnp.int32, (BLOCK, 128), 1)
+    down = jnp.where(
+        lane < count,
+        down[:BLOCK],
+        jnp.where(lane < 2 * count - BLOCK, down[BLOCK : 2 * BLOCK], down[2 * BLOCK :]),
+    )
+    levels[...] = down * across * (1.0 / cells)
 
     def smooth(a, b, c, z):
         root = jnp.sqrt(jnp.full((1, 256), weights[z], F32))
@@ -166,13 +178,16 @@
             lows.append(low)
         high = jnp.concatenate(highs, axis=1)
         low = jnp.concatenate(lows, axis=1)
-        total[...] += nt(high, jnp.concatenate([high, low], axis=0))
+        total[...] += nt(
+            jnp.concatenate([high, high, low], axis=1),
+            jnp.concatenate([high, low, high], axis=1),
+        )
 
     def flat(ref):
         return ref[...].reshape(tall, ref.shape[-1])
 
     def inner(chunk, carry):
-        for z in range(4):
+        for z in (1, 2):
             load(chunk, z).wait()
         s = [flat(field.at[chunk, z]) for z in range(4)]
         accumulate(
@@ -198,18 +213,23 @@
 
         lax.fori_loop(0, chunks, outer, 0)
 
-    whole = total[:, :tall] + 2.0 * total[:, tall:]
     keep = lax.broadcasted_iota(jnp.int32, (tall, tall), 0) % ROWS == (
         lax.broadcasted_iota(jnp.int32, (tall, tall), 1) % ROWS
     )
-    picked = jnp.sum(jnp.where(keep, whole, 0.0).reshape(count, ROWS, tall), axis=1)
-    wide = jnp.concatenate([picked[:half], picked[half:]], axis=1)
-    packed = jnp.zeros((half, 128), F32)
-    rest = wide
+    picked = jnp.sum(
+        jnp.where(keep, total[...], 0.0).reshape(count, ROWS, tall), axis=1
+    )
+    rest = jnp.concatenate(
+        [picked[:BLOCK], picked[BLOCK : 2 * BLOCK], picked[2 * BLOCK :]], axis=1
+    )
+    pieces = []
     for part in range(3):
-        piece = rest.astype(BF16)
-        rest = rest - piece.astype(F32)
-        packed += jnp.dot(piece, choose[...], preferred_element_type=F32)
+        piece = rest.astype(BF16).astype(F32)
+        rest = rest - piece
+        pieces.append(piece)
+    pieces = jnp.concatenate(pieces, axis=0).astype(BF16)
+    pieces = jnp.dot(pieces, choose[...], preferred_element_type=F32)
+    packed = pieces[:BLOCK] + pieces[BLOCK : 2 * BLOCK] + pieces[2 * BLOCK :]
 
     def reduce(value, buf, me, size, device_of, send, recv):
         buf[me] = value
@@ -282,8 +302,21 @@
 
     square_gram[...] = jnp.zeros_like(square_gram)
     value = packed[...]
-    gram = jnp.concatenate([value[:, :count], value[:, 64 : 64 + count]], axis=0)
-    square_gram[:count, :count] = gram + gram.T
+    upper = jnp.concatenate(
+        [
+            value[:, :count],
+            jnp.concatenate([value[:, :BLOCK], value[:, count : 2 * count - BLOCK]], axis=1),
+            jnp.concatenate(
+                [value[:, : 2 * BLOCK], value[:, 2 * count - BLOCK : 2 * count]], axis=1
+            ),
+        ],
+        axis=0,
+    )
+    shape = (count, count)
+    below = lax.broadcasted_iota(jnp.int32, shape, 0) // BLOCK > (
+        lax.broadcasted_iota(jnp.int32, shape, 1) // BLOCK
+    )
+    square_gram[:count, :count] = jnp.where(below, upper.T, upper)
     gram = square_gram[...]
 
     def eliminate(image, *arrays):
@@ -382,20 +415,20 @@
         name="gram",
         out_shape=(
             pltpu.VMEM(filt_shape, BF16),
-            pltpu.VMEM((count // 2, 128), F32),
+            pltpu.VMEM((BLOCK, 128), F32),
         ),
         in_specs=[hbm, hbm, hbm],
         out_specs=(vmem, vmem),
         scratch_shapes=[
             pltpu.VMEM((chunks, planes, count, ROWS, width), F32),
             pltpu.VMEM((2, chunks, count, ROWS, width), F32),
-            pltpu.VMEM((tall, 2 * tall), F32),
-            pltpu.VMEM((2 * tall, 128), BF16),
-            pltpu.VMEM((count // 2, 128), F32),
+            pltpu.VMEM((tall, tall), F32),
+            pltpu.VMEM((3 * tall, 128), BF16),
+            pltpu.VMEM((BLOCK, 128), F32),
             pltpu.VMEM((1, count), F32),
             pltpu.SMEM((planes,), F32),
-            pltpu.VMEM((8, count // 2, 128), F32),
-            pltpu.VMEM((16, count // 2, 128), F32),
+            pltpu.VMEM((8, BLOCK, 128), F32),
+            pltpu.VMEM((16, BLOCK, 128), F32),
             dma((chunks, planes)),
             dma,
             dma,

time: 98.5 us -> 97.5 us (0.990)
  no operation moved by 1% of the time
where the time goes in v4:
time: 97.5 us; the launch traced here: 97.4 us
  Pallas kernels  96.8 us (99%)
    pallas_call x1, Pallas kernels, local(): pl.pallas_call(functools.partial(gram_kernel, chunks, cells), name='gram'...  88.1 us
    pallas_call x1, Pallas kernels, local(): pl.pallas_call(functools.partial(mode_kernel, chunks), name='modes', out_...  8.64 us

profile of v4, /device:TPU:0, one launch (start us, length us, event | category | flops | bytes accessed | tf_op | source)
XLA Modules:
  0.0 97.4 jit_solution(9458869705404993366)
XLA Ops:
  0.6 0.0 copy-start
  0.6 0.0 copy-start.1
  0.6 88.1 %gram.1 = (bf16[4,8,768,256]{3,2,1,0:T(8,128)(2,1)S(1)}, f32[16,128]{1,0:T(8,128)S(1)}) custom-call(f32[48,4,64,256]{3,2,1,0:T(8,128)} %snap.1, f32[4]{0:T(128)} %weight.3, f32[1,48]{1,0:T(1,128)} %bitcast.2), custom_call_target="tpu_custom_call" | custom-call | tf_op jit(solution)/shard_map/gram/pallas_call | solution.py:413
  88.8 0.0 copy-done
  88.8 0.0 copy-done.1
  88.8 8.6 %modes.1 = (f32[16,4,64,256]{3,2,1,0:T(8,128)}, f32[16,48]{1,0:T(8,128)}) custom-call(f32[16,128]{1,0:T(8,128)S(1)} %get-tuple-element.6.packed, f32[1,48]{1,0:T(1,128)S(1)} %bitcast.3, f32[4]{0:T(128)S(1)} %copy-done, bf16[4,8,768,256]{3,2,1,0:T(8,128)(2,1)S(1)} %get-tuple-element.7.filt), custom_call_target="tpu_custom_call" | custom-call | tf_op jit(solution)/shard_map/modes/pallas_call | solution.py:450
Async XLA Ops:
  0.6 88.1 %copy-start = (f32[4]{0:T(128)S(1)}, f32[4]{0:T(128)}, u32[]{:S(2)}) copy-start(f32[4]{0:T(128)} %weight.3) | copy-start | bytes 52
  0.6 88.1 %copy-start.1 = (f32[48]{0:T(128)S(1)}, f32[48]{0:T(128)}, u32[]{:S(2)}) copy-start(f32[48]{0:T(128)} %param.4) | copy-start | bytes 580

commit v5 on v4

--- a/solution.py
+++ b/solution.py
@@ -211,7 +211,8 @@
             accumulate(chunk, (z,), [value])
             return carry
 
-        lax.fori_loop(0, chunks, outer, 0)
+        for chunk in range(chunks):
+            outer(chunk, 0)
 
     keep = lax.broadcasted_iota(jnp.int32, (tall, tall), 0) % ROWS == (
         lax.broadcasted_iota(jnp.int32, (tall, tall), 1) % ROWS
@@ -231,11 +232,11 @@
     pieces = jnp.dot(pieces, choose[...], preferred_element_type=F32)
     packed = pieces[:BLOCK] + pieces[BLOCK : 2 * BLOCK] + pieces[2 * BLOCK :]
 
-    def reduce(value, buf, me, size, device_of, send, recv):
+    def reduce(value, buf, me, size, device_of, send, recv, order, shift):
         buf[me] = value
         copies = []
-        for step in range(1, size):
-            other = lax.rem(me + step, size)
+        for offset in order:
+            other = shift(offset)
             copies.append(
                 pltpu.make_async_remote_copy(
                     src_ref=buf.at[me],
@@ -248,8 +249,8 @@
             )
         for copy in copies:
             copy.start()
-        for step in range(1, size):
-            other = lax.rem(me + step, size)
+        for offset in order:
+            other = shift(offset)
             pltpu.make_async_remote_copy(
                 src_ref=buf.at[other],
                 dst_ref=buf.at[other],
@@ -264,10 +265,17 @@
         return parts[0], copies
 
     packed, line_copies = reduce(
-        packed, line_buf, line, 8, line_device, line_send, line_recv
+        packed, line_buf, line, 8, line_device, line_send, line_recv,
+        [(1, 1, 0), (1, 0, 0), (1, 1, 1), (0, 1, 1), (1, 0, 1), (0, 0, 1), (0, 1, 0)],
+        lambda o: (lax.rem(h + o[0], 2) * 2 + lax.rem(c + o[1], 2)) * 2 + lax.rem(g + o[2], 2),
     )
     packed, plane_copies = reduce(
-        packed, plane_buf, plane, 16, plane_device, plane_send, plane_recv
+        packed, plane_buf, plane, 16, plane_device, plane_send, plane_recv,
+        sorted(
+            [(i, j) for i in range(4) for j in range(4) if i or j],
+            key=lambda o: -(min(o[0], 4 - o[0]) + min(o[1], 4 - o[1])),
+        ),
+        lambda o: lax.rem(y + o[0], 4) * 4 + lax.rem(x + o[1], 4),
     )
     gram_out[...] = packed * levels[...]
     for copy in line_copies + plane_copies:

time: 97.5 us -> 97.2 us (level)
  no operation moved by 1% of the time
where the time goes in v5:
time: 97.2 us; the launch traced here: 97.1 us
  Pallas kernels  96.4 us (99%)
    pallas_call x1, Pallas kernels, local(): pl.pallas_call(functools.partial(gram_kernel, chunks, cells), name='gram'...  87.7 us
    pallas_call x1, Pallas kernels, local(): pl.pallas_call(functools.partial(mode_kernel, chunks), name='modes', out_...  8.64 us

profile of v5, /device:TPU:0, one launch (start us, length us, event | category | flops | bytes accessed | tf_op | source)
XLA Modules:
  0.0 97.1 jit_solution(13041330498818212068)
XLA Ops:
  0.6 0.0 copy-start
  0.6 0.0 copy-start.1
  0.6 87.7 %gram.1 = (bf16[4,8,768,256]{3,2,1,0:T(8,128)(2,1)S(1)}, f32[16,128]{1,0:T(8,128)S(1)}) custom-call(f32[48,4,64,256]{3,2,1,0:T(8,128)} %snap.1, f32[4]{0:T(128)} %weight.3, f32[1,48]{1,0:T(1,128)} %bitcast.2), custom_call_target="tpu_custom_call" | custom-call | tf_op jit(solution)/shard_map/gram/pallas_call | solution.py:421
  88.4 0.0 copy-done
  88.4 0.0 copy-done.1
  88.4 8.6 %modes.1 = (f32[16,4,64,256]{3,2,1,0:T(8,128)}, f32[16,48]{1,0:T(8,128)}) custom-call(f32[16,128]{1,0:T(8,128)S(1)} %get-tuple-element.6.packed, f32[1,48]{1,0:T(1,128)S(1)} %bitcast.3, f32[4]{0:T(128)S(1)} %copy-done, bf16[4,8,768,256]{3,2,1,0:T(8,128)(2,1)S(1)} %get-tuple-element.7.filt), custom_call_target="tpu_custom_call" | custom-call | tf_op jit(solution)/shard_map/modes/pallas_call | solution.py:458
Async XLA Ops:
  0.6 87.8 %copy-start = (f32[4]{0:T(128)S(1)}, f32[4]{0:T(128)}, u32[]{:S(2)}) copy-start(f32[4]{0:T(128)} %weight.3) | copy-start | bytes 52
  0.6 87.8 %copy-start.1 = (f32[48]{0:T(128)S(1)}, f32[48]{0:T(128)}, u32[]{:S(2)}) copy-start(f32[48]{0:T(128)} %param.4) | copy-start | bytes 580

commit v6 on v5

--- a/solution.py
+++ b/solution.py
@@ -179,8 +179,8 @@
         high = jnp.concatenate(highs, axis=1)
         low = jnp.concatenate(lows, axis=1)
         total[...] += nt(
-            jnp.concatenate([high, high, low], axis=1),
-            jnp.concatenate([high, low, high], axis=1),
+            jnp.concatenate([high, high, low, low], axis=1),
+            jnp.concatenate([high, low, high, low], axis=1),
         )
 
     def flat(ref):

time: 97.2 us -> 97.3 us (level)
  no operation moved by 1% of the time
where the time goes in v6:
time: 97.3 us; the launch traced here: 97.2 us
  Pallas kernels  96.5 us (99%)
    pallas_call x1, Pallas kernels, local(): pl.pallas_call(functools.partial(gram_kernel, chunks, cells), name='gram'...  87.8 us
    pallas_call x1, Pallas kernels, local(): pl.pallas_call(functools.partial(mode_kernel, chunks), name='modes', out_...  8.64 us

profile of v6, /device:TPU:0, one launch (start us, length us, event | category | flops | bytes accessed | tf_op | source)
XLA Modules:
  0.0 97.2 jit_solution(12918344720669142710)
XLA Ops:
  0.6 0.0 copy-start
  0.6 0.0 copy-start.1
  0.6 87.8 %gram.1 = (bf16[4,8,768,256]{3,2,1,0:T(8,128)(2,1)S(1)}, f32[16,128]{1,0:T(8,128)S(1)}) custom-call(f32[48,4,64,256]{3,2,1,0:T(8,128)} %snap.1, f32[4]{0:T(128)} %weight.3, f32[1,48]{1,0:T(1,128)} %bitcast.2), custom_call_target="tpu_custom_call" | custom-call | tf_op jit(solution)/shard_map/gram/pallas_call | solution.py:421
  88.5 0.0 copy-done
  88.5 0.0 copy-done.1
  88.5 8.6 %modes.1 = (f32[16,4,64,256]{3,2,1,0:T(8,128)}, f32[16,48]{1,0:T(8,128)}) custom-call(f32[16,128]{1,0:T(8,128)S(1)} %get-tuple-element.6.packed, f32[1,48]{1,0:T(1,128)S(1)} %bitcast.3, f32[4]{0:T(128)S(1)} %copy-done, bf16[4,8,768,256]{3,2,1,0:T(8,128)(2,1)S(1)} %get-tuple-element.7.filt), custom_call_target="tpu_custom_call" | custom-call | tf_op jit(solution)/shard_map/modes/pallas_call | solution.py:458
Async XLA Ops:
  0.6 87.9 %copy-start = (f32[4]{0:T(128)S(1)}, f32[4]{0:T(128)}, u32[]{:S(2)}) copy-start(f32[4]{0:T(128)} %weight.3) | copy-start | bytes 52
  0.6 87.9 %copy-start.1 = (f32[48]{0:T(128)S(1)}, f32[48]{0:T(128)}, u32[]{:S(2)}) copy-start(f32[48]{0:T(128)} %param.4) | copy-start | bytes 580
